TPU v7x, 32 devices: a whole 2x2x4 slice. The times are simulated.
32 devices in a mesh: groups: 2 (over x), patch: 16 (over z, y, core).
Axes of the slice: x: 2, y: 2, z: 4, core: 2. Of those that a mesh axis runs over, the one named last changes fastest.
Arguments:
- tokens: bfloat16 [16384, 1152], P(('groups', 'patch')), parts along dimension 0, may hold values from -6 to 6
- stale_kv: bfloat16 [16384, 1152], P(('groups', 'patch')), parts along dimension 0, may hold values from -40 to 40, as said below
- mod_table: float32 [6, 1152], replicated, may hold values from -2 to 3
- mod_mix: float32 [6, 1152], replicated, may hold values from -3 to 3
- timestep: int32 [2], P('groups'), parts along dimension 0, may hold values from 0 to 999
- frame_order: int32 [8], P('groups'), parts along dimension 0, may hold values from 0 to 3, each once
- spatial_qkv: bfloat16 [3, 1152, 576], replicated, may hold values from -0.1875 to 0.1875
- spatial_out: bfloat16 [576, 1152], replicated, may hold values from -0.25 to 0.25
- temporal_qkv: bfloat16 [3, 1152, 576], replicated, may hold values from -0.1875 to 0.1875
- temporal_out: bfloat16 [576, 1152], replicated, may hold values from -0.25 to 0.25
Outputs:
- block_out: float32 [16384, 1152], P(('groups', 'patch')), parts along dimension 0
There are 2 independent parts, one for each index of `groups`. A program takes and returns all parts, laid end to end along the dimension named above; an argument that names none is the same for every part. Nothing has to cross between parts.
Inputs may be any that keep to these rules, and one draw needn't show every extreme that they name: `frame_order`: a permutation of the 4 time positions. `stale_kv`: previous step's keys and values.
All inputs are finite; a program needn't handle non-finite values.
Results may differ from a plain program's by a relative error of at most 0.013.
The roundings to bfloat16 on the way count: a program that leaves them out, or rounds other values in their place, can miss the bound.
Values may be sent and summed in bfloat16 or wider, within the bound.
No kernel may reach another device: no remote copies, remote signals or barrier semaphores. Data moves between devices by JAX's collectives and lax.ppermute only.
A program may use at most 128 MiB of HBM per device.

v0:
```python
import math

import jax
import jax.numpy as jnp
from jax import lax
from jax.sharding import PartitionSpec as P

HEADS = 16


epsilon = 1e-06


def from_partner(value, axis, distance):
    mask = 2**distance
    pairs = [(source, source ^ mask) for source in range(lax.axis_size(axis))]
    return lax.ppermute(value, axis, pairs)


def normalize(activations):
    row_mean = jnp.mean(activations, axis=-1, keepdims=True)
    centered = activations - row_mean
    variance = jnp.mean(centered * centered, axis=-1, keepdims=True)
    return centered * lax.rsqrt(variance + epsilon)


def sinusoid(position, feature_width):
    half_width = feature_width // 2
    frequencies = jnp.exp(
        -math.log(10000.0) * jnp.arange(half_width, dtype=jnp.float32) / half_width
    )
    angles = jnp.asarray(position).astype(jnp.float32)[..., None] * frequencies
    return jnp.concatenate([jnp.sin(angles), jnp.cos(angles)], axis=-1)


def softmax_rows(scores):
    row_top = jnp.max(scores, axis=-1, keepdims=True)
    exp_scores = jnp.exp(scores - row_top)
    return (exp_scores / jnp.sum(exp_scores, axis=-1, keepdims=True)).astype(jnp.bfloat16)


def spatial_attend(queries, key_rows, value_rows, head_dim):
    width_win = queries.shape[1]
    head_count = width_win // head_dim
    query_heads = queries.reshape(-1, head_count, head_dim)
    key_heads = key_rows.reshape(-1, head_count, head_dim)
    value_heads = value_rows.reshape(-1, head_count, head_dim)
    scores = jnp.einsum(
        "qhe,khe->hqk", query_heads, key_heads, preferred_element_type=jnp.float32
    ) * head_dim ** (-0.5)
    weights = softmax_rows(scores)
    mixed_out = jnp.einsum("hqk,khe->qhe", weights, value_heads, preferred_element_type=jnp.float32)
    return mixed_out.reshape(-1, width_win).astype(jnp.bfloat16)


def temporal_attend(queries, key_rows, value_rows, head_dim):
    frame_count, pixel_count, width_win = queries.shape
    head_count = width_win // head_dim
    shape_heads = (frame_count, pixel_count, head_count, head_dim)
    query_heads = queries.reshape(shape_heads)
    key_heads = key_rows.reshape(shape_heads)
    value_heads = value_rows.reshape(shape_heads)
    scores = jnp.einsum(
        "fmhe,gmhe->mhfg", query_heads, key_heads, preferred_element_type=jnp.float32
    ) * head_dim ** (-0.5)
    weights = softmax_rows(scores)
    mixed_out = jnp.einsum(
        "mhfg,gmhe->fmhe", weights, value_heads, preferred_element_type=jnp.float32
    )
    return mixed_out.reshape(frame_count, pixel_count, width_win).astype(jnp.bfloat16)


def per_device(
    tokens,
    stale_kv,
    mod_table,
    mod_mix,
    timestep,
    frame_order,
    spatial_qkv,
    spatial_out,
    temporal_qkv,
    temporal_out,
):
    devices = lax.axis_size("patch")
    dev_index = lax.axis_index("patch")
    frames = devices // 4
    quarter = dev_index % 4
    frame_slot = dev_index // 4
    row_count, feature_width = tokens.shape
    width_win = spatial_out.shape[0]
    head_dim = feature_width // HEADS
    modulation = mod_table + mod_mix * sinusoid(timestep[0], feature_width)[None, :]
    tokens_wide = tokens.astype(jnp.float32)
    spatial_in = (normalize(tokens_wide) * (1.0 + modulation[1]) + modulation[0]).astype(
        jnp.bfloat16
    )
    fresh_qkv = jnp.einsum(
        "tr,jrd->jtd", spatial_in, spatial_qkv, preferred_element_type=jnp.float32
    ).astype(jnp.bfloat16)
    bit_order = (0, 1)
    kv_block = stale_kv
    for bit_num in bit_order:
        partner = from_partner(kv_block, "patch", bit_num)
        low_half = dev_index >> bit_num & 1 == 0
        kv_block = jnp.where(
            low_half, jnp.stack([kv_block, partner], 0), jnp.stack([partner, kv_block], 0)
        )
    kv_block = kv_block.reshape(4, row_count, 2 * width_win)
    own_mask = (jnp.arange(4) == quarter)[:, None, None]
    key_rows = jnp.where(own_mask, fresh_qkv[1][None], kv_block[:, :, :width_win]).reshape(
        4 * row_count, width_win
    )
    value_rows = jnp.where(own_mask, fresh_qkv[2][None], kv_block[:, :, width_win:]).reshape(
        4 * row_count, width_win
    )
    spatial_mixed = spatial_attend(fresh_qkv[0], key_rows, value_rows, head_dim)
    spatial_proj = jnp.dot(spatial_mixed, spatial_out, preferred_element_type=jnp.float32)
    after_spatial = tokens_wide + modulation[2] * spatial_proj
    frame_id = jnp.sum(jnp.where(jnp.arange(frames) == frame_slot, frame_order, 0))
    temporal_in = (
        normalize(after_spatial) * (1.0 + modulation[4])
        + modulation[3]
        + sinusoid(frame_id, feature_width)[None, :]
    ).astype(jnp.bfloat16)
    piece_rows = row_count // devices
    arriving = lax.all_to_all(
        temporal_in.reshape(devices, piece_rows, feature_width),
        "patch",
        split_axis=0,
        concat_axis=0,
        tiled=True,
    )
    arranged = arriving.reshape(frames, 4 * piece_rows, feature_width)
    flat_rows = arranged.reshape(-1, feature_width)
    temporal_proj = jnp.einsum(
        "tr,jrd->jtd", flat_rows, temporal_qkv, preferred_element_type=jnp.float32
    )
    temporal_proj = temporal_proj.astype(jnp.bfloat16).reshape(
        (3,) + arranged.shape[:-1] + (width_win,)
    )
    mixed_out = temporal_attend(temporal_proj[0], temporal_proj[1], temporal_proj[2], head_dim)
    returning = lax.all_to_all(
        mixed_out.reshape(devices, piece_rows, width_win),
        "patch",
        split_axis=0,
        concat_axis=0,
        tiled=True,
    )
    temporal_mixed = returning.reshape(row_count, width_win)
    temporal_proj_out = jnp.dot(temporal_mixed, temporal_out, preferred_element_type=jnp.float32)
    return after_spatial + modulation[5] * temporal_proj_out


def solution(mesh):
    return jax.shard_map(
        per_device,
        mesh=mesh,
        in_specs=(
            P(("groups", "patch"), None),
            P(("groups", "patch"), None),
            P(),
            P(),
            P("groups"),
            P("groups"),
            P(),
            P(),
            P(),
            P(),
        ),
        out_specs=P(("groups", "patch"), None),
        check_vma=False,
    )
```

profile of v0, /device:TPU:0, one launch (start us, length us, event | category | flops | bytes accessed | tf_op | source)
XLA Modules:
  0.0 210.0 jit_solution(12419421594038518087)
XLA Ops:
  0.0 0.5 collective-permute-start
  1.2 0.1 pad_maximum_fusion
  1.3 1.5 convert_reduce_fusion
  2.8 0.8 multiply_add_fusion
  3.6 0.0 collective-permute-done
  3.6 3.9 %maximum_select_fusion.2 = bf16[2,512,1152]{2,1,0:T(8,128)(2,1)} fusion(bf16[1,512,1152]{2,1,0:T(8,128)(2,1)S(1)} %bitcast.59, bf16[1,512,1152]{2,1,0:T(8,128)(2,1)} %bitcast.57, pred[]{:T(512)S(6)} %eq.27), kind=kLoop, calls=%fused_computation.24 | loop fusion | flops 3538944 | bytes 4718593 | tf_op jit(solution)/shard_map/jit(_where)/select_n | solution.py:106
  7.5 2.6 %collective-permute-start.1 = (bf16[2,512,1152]{2,1,0:T(8,128)(2,1)}, bf16[2,512,1152]{2,1,0:T(8,128)(2,1)}, u32[]{:S(2)}, u32[]{:S(2)}) collective-permute-start(bf16[2,512,1152]{2,1,0:T(8,128)(2,1)} %maximum_select_fusion.2), channel_id=1, source_target_pairs={{0,2},{1,3},{2,0},{3,1},{4,6},{5,7},{6,4},{7,5},{8,10},{9,11},{10,... | collective-permute-start | bytes 7077896 | tf_op jit(solution)/shard_map/ppermute | solution.py:17
  10.1 0.6 slice_reduce_fusion.1
  10.7 1.7 fusion.10
  12.4 5.2 %convert_bitcast_fusion.1 = bf16[3,512,576]{1,2,0:T(8,128)(2,1)S(1)} fusion(bf16[3,1152,576]{1,2,0:T(8,128)(2,1)} %param.16, bf16[512,1152]{1,0:T(8,128)(2,1)} %param.10, f32[1152]{0:T(1024)S(1)} %get-tuple-element.8, f32[1152]{0:T(1024)S(1)} %get-tuple-element.9, f32[512]{0:T(512)S(1)} %add_rsqrt_fusion.1, f32[512]{0:T(512)S(1)} %broadcast_multiply_fusion.1), kind=kOutput, calls=%fused_computation.33 | convolution fusion | flops 2042855424 | bytes 6943744 | tf_op jit(solution)/shard_map/tr,jrd->jtd/dot_general | solution.py:98
  17.6 0.0 copy-start.11
  17.6 0.0 copy-start.2
  17.6 1.3 slice_bitcast_fusion
  18.9 1.4 copy.21
  20.3 2.2 %copy.19 = bf16[512,576]{1,0:T(8,128)(2,1)} copy(bf16[512,576]{0,1:T(8,128)(2,1)} %get-tuple-element.18) | data formatting | bytes 1179648 | tf_op jit(solution)/shard_map/jit(_where)/broadcast_in_dim | solution.py:114
  22.4 0.6 fusion.34
  23.7 0.1 fusion.32
  23.8 0.1 pad_maximum_fusion.1
  23.9 2.0 maximum_select_fusion.1
  25.9 36.3 %collective-permute-done.1 = bf16[2,512,1152]{2,1,0:T(8,128)(2,1)} collective-permute-done((bf16[2,512,1152]{2,1,0:T(8,128)(2,1)}, bf16[2,512,1152]{2,1,0:T(8,128)(2,1)}, u32[]{:S(2)}, u32[]{:S(2)}) %collective-permute-start.1) | collective-permute-done | bytes 2359328 | tf_op jit(solution)/shard_map/ppermute | solution.py:17
  62.2 3.1 %maximum_select_fusion = bf16[2,2,512,1152]{3,2,1,0:T(8,128)(2,1)S(1)} fusion(bf16[1,2,512,1152]{3,2,1,0:T(8,128)(2,1)} %bitcast.8, bf16[1,2,512,1152]{3,2,1,0:T(8,128)(2,1)S(1)} %maximum_select_fusion.1, pred[]{:T(512)S(6)} %eq.26), kind=kLoop, calls=%fused_computation.8 | loop fusion | flops 7077888 | bytes 9437185 | tf_op jit(solution)/shard_map/jit(_where)/select_n | solution.py:106
  65.3 3.4 %slice_select_fusion = (bf16[4,512,576]{2,1,0:T(8,128)(2,1)}, bf16[4,512,576]{2,1,0:T(8,128)(2,1)}) fusion(bf16[4,512,1152]{2,1,0:T(8,128)(2,1)S(1)} %bitcast.56, pred[4]{0:T(512)(128)(4,1)S(1)} %iota_compare_fusion, bf16[512,576]{1,0:T(8,128)(2,1)S(1)} %copy.21, bf16[512,576]{1,0:T(8,128)(2,1)S(1)} %copy-done.5), kind=kLoop, calls=%fused_computation.17 | loop fusion | flops 2359296 | bytes 10616836 | tf_op jit(solution)/shard_map/jit(_where)/select_n | solution.py:111
  68.7 5.4 %copy.20 = bf16[4,512,576]{1,0,2:T(4,128)(2,1)} copy(bf16[4,512,576]{2,1,0:T(8,128)(2,1)} %get-tuple-element.12) | data formatting | bytes 4718592 | tf_op jit(solution)/shard_map/jit(_where)/select_n | solution.py:114
  74.1 5.8 %reshape_reshape.9 = bf16[2048,8,72]{0,2,1:T(8,128)(2,1)} reshape(bf16[4,512,576]{1,0,2:T(4,128)(2,1)} %copy.20) | data formatting | bytes 4718592 | tf_op jit(solution)/shard_map/reshape;reshape | solution.py:47
  80.0 5.4 %copy.22 = bf16[4,512,576]{1,0,2:T(4,128)(2,1)} copy(bf16[4,512,576]{2,1,0:T(8,128)(2,1)} %get-tuple-element.11) | data formatting | bytes 4718592 | tf_op jit(solution)/shard_map/jit(_where)/select_n | solution.py:111
  85.4 5.9 %reshape_reshape.10 = bf16[2048,8,72]{0,2,1:T(8,128)(2,1)} reshape(bf16[4,512,576]{1,0,2:T(4,128)(2,1)} %copy.22) | data formatting | bytes 4718592 | tf_op jit(solution)/shard_map/reshape;reshape | solution.py:46
  91.4 17.3 %fusion.38 = (f32[8,512]{1,0:T(8,128)S(1)}, f32[8,512,2048]{2,1,0:T(8,128)}) fusion(bf16[512,8,72]{0,2,1:T(8,128)(2,1)S(1)} %bitcast.64, bf16[2048,8,72]{0,2,1:T(8,128)(2,1)} %reshape_reshape.10), kind=kOutput, calls=%fused_computation.73 | convolution fusion | flops 1233127424 | bytes 36519936 | tf_op jit(solution)/shard_map/sub | solution.py:38
  108.7 14.1 %fusion.18 = bf16[8,72,512]{2,1,0:T(8,128)(2,1)S(1)} fusion(bf16[2048,8,72]{0,2,1:T(8,128)(2,1)} %reshape_reshape.9, f32[8,512,2048]{2,1,0:T(8,128)} %get-tuple-element.20, f32[8,512]{1,0:T(8,128)S(1)} %get-tuple-element.19), kind=kOutput, calls=%fused_computation.36 | convolution fusion | flops 1225031680 | bytes 36519936 | tf_op jit(solution)/shard_map/hqk,khe->qhe/dot_general | solution.py:52
  122.8 1.4 fusion.39
  124.2 0.4 multiply_reduce_fusion.1
  124.6 0.0 copy-start.10
  124.6 0.5 add_convert_fusion
  125.2 0.5 copy-done.1
  125.6 35.6 %all_to_all.10 = bf16[16,32,1152]{2,1,0:T(8,128)(2,1)S(1)} all-to-all(bf16[16,32,1152]{2,1,0:T(8,128)(2,1)S(1)} %bitcast.61), channel_id=1, replica_groups=mesh['groups'=2,'patch'=16] {'patch'}, dimensions={0} | all-to-all | bytes 2359296 | tf_op jit(solution)/shard_map/all_to_all | solution.py:127
  161.2 2.5 %convert_bitcast_fusion = bf16[3,512,576]{1,2,0:T(8,128)(2,1)S(1)} fusion(bf16[512,1152,1]{1,0,2:T(8,128)(2,1)S(1)} %bitcast.63, bf16[3,1152,576]{1,2,0:T(8,128)(2,1)S(1)} %copy-done.10), kind=kOutput, calls=%fused_computation.32 | convolution fusion | flops 2039316480 | bytes 6930432 | tf_op jit(solution)/shard_map/tr,jrd->jtd/dot_general | solution.py:136
  163.8 0.1 fusion.37
  163.9 0.9 reshape_squeeze.13
  164.9 3.4 %copy.25 = bf16[4,128,8,72]{3,0,2,1:T(4,128)(2,1)} copy(bf16[4,128,8,72]{1,0,3,2:T(4,128)(2,1)} %reshape_squeeze.13) | data formatting | bytes 1179648 | tf_op jit(solution)/shard_map/reshape;squeeze | solution.py:62
  168.2 0.1 reshape_squeeze.14
  168.4 2.4 %copy.23 = bf16[4,128,8,72]{3,0,2,1:T(4,128)(2,1)} copy(bf16[4,128,8,72]{1,0,3,2:T(4,128)(2,1)S(1)} %reshape_squeeze.14) | data formatting | bytes 1179648 | tf_op jit(solution)/shard_map/reshape;squeeze | solution.py:60
  170.8 0.1 reshape_squeeze.15
  170.9 2.4 %copy.24 = bf16[4,128,8,72]{3,0,2,1:T(4,128)(2,1)} copy(bf16[4,128,8,72]{1,0,3,2:T(4,128)(2,1)S(1)} %reshape_squeeze.15) | data formatting | bytes 1179648 | tf_op jit(solution)/shard_map/reshape;squeeze | solution.py:61
  173.3 6.7 %fusion.40 = (f32[128,8,4]{2,1,0:T(8,128)}, f32[128,8,4,4]{2,3,1,0:T(4,128)}) fusion(bf16[4,128,8,72]{3,0,2,1:T(4,128)(2,1)S(1)} %copy-done.7, bf16[4,128,8,72]{3,0,2,1:T(4,128)(2,1)} %copy.24), kind=kOutput, calls=%fused_computation.75 | convolution fusion | flops 2408451 | bytes 1261568 | tf_op jit(solution)/shard_map/sub | solution.py:38
  180.0 2.9 %fusion.17 = bf16[4,128,8,72]{3,0,2,1:T(4,128)(2,1)S(1)} fusion(bf16[4,128,8,72]{3,0,2,1:T(4,128)(2,1)S(1)} %copy-done.6, f32[128,8,4,4]{2,3,1,0:T(4,128)} %get-tuple-element.24, f32[128,8,4]{2,1,0:T(8,128)} %get-tuple-element.23), kind=kOutput, calls=%fused_computation.35 | convolution fusion | flops 2686976 | bytes 1261568 | tf_op jit(solution)/shard_map/mhfg,gmhe->fmhe/dot_general | solution.py:67
  183.0 0.1 copy.27
  183.1 0.8 convert_element_type.72
  184.0 21.3 %all_to_all.11 = bf16[16,32,576]{2,1,0:T(8,128)(2,1)S(1)} all-to-all(bf16[16,32,576]{2,1,0:T(8,128)(2,1)S(1)} %convert_element_type.72), channel_id=1, replica_groups=mesh['groups'=2,'patch'=16] {'patch'}, dimensions={0} | all-to-all | bytes 1179648 | tf_op jit(solution)/shard_map/all_to_all | solution.py:143
  205.3 4.7 %fusion.7 = f32[512,1152]{1,0:T(8,128)} fusion(f32[512,1152]{1,0:T(8,128)} %copy-done.1, bf16[512,576]{1,0:T(8,128)(2,1)S(1)} %bitcast.62, bf16[576,1152]{1,0:T(8,128)(2,1)} %param.19, f32[1152]{0:T(1024)S(1)} %copy-done.9), kind=kOutput, calls=%fused_computation.14 | convolution fusion | flops 680656896 | bytes 6640128 | tf_op jit(solution)/shard_map/dot_general | solution.py:151
  (26 shorter events, 0.1 us)
Async XLA Ops:
  0.0 122.8 %copy-start = (bf16[576,1152]{1,0:T(8,128)(2,1)S(1)}, bf16[576,1152]{1,0:T(8,128)(2,1)}, u32[]{:S(2)}) copy-start(bf16[576,1152]{1,0:T(8,128)(2,1)} %param.17) | copy-start | bytes 3981316
  0.0 3.6 %collective-permute-start = (bf16[512,1152]{1,0:T(8,128)(2,1)}, bf16[512,1152]{1,0:T(8,128)(2,1)S(1)}, u32[]{:S(2)}, u32[]{:S(2)}) collective-permute-start(bf16[512,1152]{1,0:T(8,128)(2,1)} %param.11), channel_id=1, source_target_pairs={{0,1},{1,0},{2,3},{3,2},{4,5},{5,4},{6,7},{7,6},{8,9},{9,8},{10,11... | collective-permute-start | bytes 3538952 | tf_op jit(solution)/shard_map/ppermute | solution.py:17
  3.6 3.9 %copy-start.3 = (bf16[512,1152]{1,0:T(8,128)(2,1)}, bf16[512,1152]{1,0:T(8,128)(2,1)S(1)}, u32[]{:S(2)}) copy-start(bf16[512,1152]{1,0:T(8,128)(2,1)S(1)} %collective-permute-done) | copy-start | bytes 3538948
  7.5 54.7 %collective-permute-start.1 = (bf16[2,512,1152]{2,1,0:T(8,128)(2,1)}, bf16[2,512,1152]{2,1,0:T(8,128)(2,1)}, u32[]{:S(2)}, u32[]{:S(2)}) collective-permute-start(bf16[2,512,1152]{2,1,0:T(8,128)(2,1)} %maximum_select_fusion.2), channel_id=1, source_target_pairs={{0,2},{1,3},{2,0},{3,1},{4,6},{5,7},{6,4},{7,5},{8,10},{9,11},{10,... | collective-permute-start | bytes 7077896 | tf_op jit(solution)/shard_map/ppermute | solution.py:17
  17.6 4.8 %copy-start.11 = (s32[4]{0:T(128)S(1)}, s32[4]{0:T(128)}, u32[]{:S(2)}) copy-start(s32[4]{0:T(128)} %param.15) | copy-start | bytes 52
  17.6 6.2 %copy-start.2 = (bf16[512,1152]{1,0:T(8,128)(2,1)S(1)}, bf16[512,1152]{1,0:T(8,128)(2,1)}, u32[]{:S(2)}) copy-start(bf16[512,1152]{1,0:T(8,128)(2,1)} %param.11) | copy-start | bytes 3538948
  62.2 3.1 %copy-start.5 = (bf16[512,576]{1,0:T(8,128)(2,1)S(1)}, bf16[512,576]{1,0:T(8,128)(2,1)}, u32[]{:S(2)}) copy-start(bf16[512,576]{1,0:T(8,128)(2,1)} %copy.19) | copy-start | bytes 1769476
  85.4 5.9 %copy-start.8 = (bf16[1,512,576]{1,2,0:T(8,128)(2,1)S(1)}, bf16[1,512,576]{1,2,0:T(8,128)(2,1)}, u32[]{:S(2)}) copy-start(bf16[1,512,576]{1,2,0:T(8,128)(2,1)} %get-tuple-element.17) | copy-start | bytes 1769476
  108.6 14.1 %copy-start.4 = (bf16[512,1152]{1,0:T(8,128)(2,1)S(1)}, bf16[512,1152]{1,0:T(8,128)(2,1)}, u32[]{:S(2)}) copy-start(bf16[512,1152]{1,0:T(8,128)(2,1)} %param.10) | copy-start | bytes 3538948
  124.2 1.4 copy-start.1
  124.6 36.6 %copy-start.10 = (bf16[3,1152,576]{1,2,0:T(8,128)(2,1)S(1)}, bf16[3,1152,576]{1,2,0:T(8,128)(2,1)}, u32[]{:S(2)}) copy-start(bf16[3,1152,576]{1,2,0:T(8,128)(2,1)} %param.18) | copy-start | bytes 11943940
  170.8 2.5 %copy-start.7 = (bf16[4,128,8,72]{3,0,2,1:T(4,128)(2,1)S(1)}, bf16[4,128,8,72]{3,0,2,1:T(4,128)(2,1)}, u32[]{:S(2)}) copy-start(bf16[4,128,8,72]{3,0,2,1:T(4,128)(2,1)} %copy.23) | copy-start | bytes 1769476
  173.3 6.7 %copy-start.6 = (bf16[4,128,8,72]{3,0,2,1:T(4,128)(2,1)S(1)}, bf16[4,128,8,72]{3,0,2,1:T(4,128)(2,1)}, u32[]{:S(2)}) copy-start(bf16[4,128,8,72]{3,0,2,1:T(4,128)(2,1)} %copy.25) | copy-start | bytes 1769476
  183.0 22.3 %copy-start.9 = (f32[1152]{0:T(1024)S(1)}, f32[1152]{0:T(1024)}, u32[]{:S(2)}) copy-start(f32[1152]{0:T(1024)} %get-tuple-element.5) | copy-start | bytes 13828
where the time goes:
time: 211 us; the launch traced here: 210 us
  blocking collectives  56.9 us (27%)
  matrix products  54.9 us (26%)
  local copies, waits for them, and re-layouts  38.4 us (18%)
  waiting for transfers between devices  36.3 us (17%)
  other arithmetic  18.9 us (9%)
  starting transfers between devices  3.11 us (1%)
    ppermute x2, waiting for transfers between devices, from_partner(): return lax.ppermute(value, axis, pairs)  36.3 us
    all_to_all x1, blocking collectives, per_device(): lax.all_to_all(temporal_in.reshape(devices, piece_rows, feature_width), '...  35.6 us
    sub x2, matrix products, softmax_rows(): exp_scores = jnp.exp(scores - row_top)  24 us
    all_to_all x1, blocking collectives, per_device(): lax.all_to_all(mixed_out.reshape(devices, piece_rows, width_win), 'patch'...  21.3 us
    dot_general x1, matrix products, spatial_attend(): jnp.einsum('hqk,khe->qhe', weights, value_heads, preferred_element_type=j...  14.1 us
    select_n x3, other arithmetic, per_device(): jnp.where(low_half, jnp.stack([kv_block, partner], 0), jnp.stack([partner...  8.99 us
    another operation x1, local copies, waits for them, and re-layouts, spatial_attend(): key_heads = key_rows.reshape(-1, head_count, head_dim)  5.92 us
    another operation x1, local copies, waits for them, and re-layouts, spatial_attend(): value_heads = value_rows.reshape(-1, head_count, head_dim)  5.85 us
  transfers between devices with their start and end apart: 2, of which 1 were waited for; matrix products, arithmetic and copies ran while one was open for 8% of the time, Pallas kernels for 0%

commit v1 on v0

v1 whole, which is shorter than its diff:
```python
import functools
import math

import jax
import jax.numpy as jnp
from jax import lax
from jax.experimental import pallas as pl
from jax.experimental.pallas import tpu as pltpu
from jax.sharding import PartitionSpec as P

HEADS = 16
LANES = 128
QUERY_ROWS = 128
PAIR_GROUPS = ((0, 1), (2,), (3,))
HALVES = 2

epsilon = 1e-06
bf16 = jnp.bfloat16
f32 = jnp.float32
NT = (((1,), (1,)), ((), ()))


def permute(value, target):
    count = lax.axis_size("patch")
    return lax.ppermute(value, "patch", [(source, target(source)) for source in range(count)])


def normalize(activations):
    row_mean = jnp.mean(activations, axis=-1, keepdims=True)
    centered = activations - row_mean
    variance = jnp.mean(centered * centered, axis=-1, keepdims=True)
    return centered * lax.rsqrt(variance + epsilon)


def sinusoid(position, feature_width):
    half_width = feature_width // 2
    frequencies = jnp.exp(
        -math.log(10000.0) * jnp.arange(half_width, dtype=jnp.float32) / half_width
    )
    angles = jnp.asarray(position).astype(jnp.float32)[..., None] * frequencies
    return jnp.concatenate([jnp.sin(angles), jnp.cos(angles)], axis=-1)


def column_mask(first, width, dtype):
    column = lax.broadcasted_iota(jnp.int32, (1, 2 * LANES), 1)
    inside = jnp.logical_and(column >= first, column < first + width)
    return jnp.where(inside, 1.0, 0.0).astype(dtype)


def softmax_scale(head_dim):
    return math.log2(math.e) * head_dim ** (-0.5)


def vmem_specs(count):
    return [pl.BlockSpec(memory_space=pltpu.VMEM) for _ in range(count)]


def pair_plan(width, head_dim):
    plan = []
    for first in range(0, width, 2 * head_dim):
        key_tile = first // LANES
        value_tile = (width + first) // LANES
        plan.append(
            (key_tile, first - key_tile * LANES, value_tile, width + first - value_tile * LANES)
        )
    return plan


def group_tiles(width, head_dim):
    plan = pair_plan(width, head_dim)
    seen, groups = set(), []
    for group in PAIR_GROUPS:
        need = []
        for pair in group:
            key_tile, _, value_tile, _ = plan[pair]
            need += [key_tile, key_tile + 1, value_tile, value_tile + 1]
        fresh = sorted(set(need) - seen)
        seen |= set(fresh)
        groups.append(tuple(fresh))
    return groups


def spatial_kernel(*refs, group, frames, head_dim, width, tiles, last):
    plan = pair_plan(width, head_dim)
    count = len(tiles)
    position = 0
    query_ref, own_ref, peer_ref = refs[:3]
    near_refs = refs[3 : 3 + count]
    far_refs = refs[3 + count : 3 + 2 * count]
    position = 3 + 2 * count
    first = group[0] == 0
    carry_ref = None
    if not first:
        carry_ref = refs[position]
        position += 1
    out_refs = refs[position : position + frames]
    carry_out = None if last else refs[position + frames]

    where = {tile: (c, j) for c, chunk in enumerate(tiles) for j, tile in enumerate(chunk)}

    def from_chunks(chunk_refs):
        def load(tile):
            chunk, at = where[tile]
            return chunk_refs[chunk][:, at * LANES : (at + 1) * LANES]

        return load

    def from_whole(ref):
        return lambda tile: ref[:, tile * LANES : (tile + 1) * LANES]

    blocks = [from_whole(own_ref), from_whole(peer_ref), from_chunks(near_refs), from_chunks(far_refs)]
    rows = query_ref.shape[0]
    scale = softmax_scale(head_dim)
    piece = rows // frames

    def two(block, tile):
        return jnp.concatenate([block(tile), block(tile + 1)], axis=1)

    def scores_of(pair, chunk):
        key_tile, key_lane, _, _ = plan[pair]
        window = query_ref[
            chunk * QUERY_ROWS : (chunk + 1) * QUERY_ROWS, key_tile * LANES : (key_tile + 2) * LANES
        ]
        stacked = jnp.concatenate(
            [
                window * column_mask(key_lane, head_dim, bf16),
                window * column_mask(key_lane + head_dim, head_dim, bf16),
            ],
            axis=0,
        )
        return [
            lax.dot_general(stacked, two(block, key_tile), NT, preferred_element_type=f32)
            for block in blocks
        ]

    def mix(pair, scores):
        _, key_lane, value_tile, value_lane = plan[pair]
        top = functools.reduce(jnp.maximum, [jnp.max(s, axis=-1, keepdims=True) for s in scores])
        top = top * scale
        weights = [jnp.exp2(s * scale - top) for s in scores]
        total = functools.reduce(jnp.add, [jnp.sum(w, axis=-1, keepdims=True) for w in weights])
        mixed = functools.reduce(
            jnp.add,
            [
                jnp.dot(w.astype(bf16), two(block, value_tile), preferred_element_type=f32)
                for w, block in zip(weights, blocks)
            ],
        )
        mixed = mixed / total
        joined = mixed[:QUERY_ROWS] * column_mask(value_lane, head_dim, f32) + mixed[
            QUERY_ROWS:
        ] * column_mask(value_lane + head_dim, head_dim, f32)
        return pltpu.roll(joined, (key_lane - value_lane) % (2 * LANES), 1)

    chunks = rows // QUERY_ROWS
    tasks = [(chunk, pair) for chunk in range(chunks) for pair in group]
    pending = scores_of(tasks[0][1], tasks[0][0])
    first_tile = plan[group[0]][0]
    parts = {}
    for index, (chunk, pair) in enumerate(tasks):
        scores = pending
        if index + 1 < len(tasks):
            pending = scores_of(tasks[index + 1][1], tasks[index + 1][0])
        joined = mix(pair, scores)
        tile = plan[pair][0]
        for side in range(2):
            half = joined[:, side * LANES : (side + 1) * LANES]
            parts[tile + side] = parts[tile + side] + half if tile + side in parts else half
        if pair != group[-1]:
            continue
        at = chunk * QUERY_ROWS
        if carry_ref is not None:
            parts[first_tile] = parts[first_tile] + carry_ref[at : at + QUERY_ROWS, :].astype(f32)
        done = sorted(parts)
        if carry_out is not None:
            carry_out[at : at + QUERY_ROWS, :] = parts[done[-1]].astype(bf16)
            done = done[:-1]
        values = jnp.concatenate([parts[tile] for tile in done], axis=1).astype(bf16)
        width_out = out_refs[0].shape[1]
        for sub in range(QUERY_ROWS // piece):
            out_refs[at // piece + sub][...] = values[sub * piece : (sub + 1) * piece, :width_out]
        parts = {}


def spatial_group(number, query, own_kv, peer_kv, near, far, carry, frames, head_dim, width):
    group = PAIR_GROUPS[number]
    last = number == len(PAIR_GROUPS) - 1
    plan = pair_plan(width, head_dim)
    tiles = tuple(group_tiles(width, head_dim)[: number + 1])
    rows = query.shape[0]
    first_column = plan[group[0]][0] * LANES
    end_column = width if last else (plan[group[-1]][0] + 1) * LANES
    columns = end_column - first_column
    out_shape = [jax.ShapeDtypeStruct((rows // frames, columns), bf16) for _ in range(frames)]
    if not last:
        out_shape.append(jax.ShapeDtypeStruct((rows, LANES), bf16))
    operands = [query, own_kv, peer_kv, *near[: number + 1], *far[: number + 1]]
    if carry is not None:
        operands.append(carry)
    keys = 4 * rows
    results = pl.pallas_call(
        functools.partial(
            spatial_kernel,
            group=group,
            frames=frames,
            head_dim=head_dim,
            width=width,
            tiles=tiles,
            last=last,
        ),
        out_shape=out_shape,
        in_specs=vmem_specs(len(operands)),
        out_specs=vmem_specs(len(out_shape)),
        cost_estimate=pl.CostEstimate(
            flops=len(group) * 2 * rows * keys * 256 * 4,
            bytes_accessed=4 * rows * 512 * 2,
            transcendentals=len(group) * 2 * rows * keys,
        ),
        name=f"spatial_{number}",
    )(*operands)
    return list(results[:frames]), (None if last else results[frames])


def temporal_kernel(*refs, frames, head_dim, groups):
    tokens_refs = refs[:frames]
    mixed_refs = refs[frames : frames + frames * groups]
    position = frames + frames * groups
    out_weight, qkv_weight, modulation_ref, place_ref = refs[position : position + 4]
    out_refs = refs[position + 4 : position + 4 + frames]
    query_ref, key_ref, value_ref = refs[position + 4 + frames :]
    piece, feature_width = tokens_refs[0].shape
    width = out_weight.shape[0]
    rows = frames * piece

    tokens_wide = jnp.concatenate([ref[...] for ref in tokens_refs], axis=0).astype(f32)
    mixed = jnp.concatenate(
        [
            jnp.concatenate([mixed_refs[frame * groups + g][...] for g in range(groups)], axis=1)
            for frame in range(frames)
        ],
        axis=0,
    )
    after = tokens_wide + modulation_ref[2:3, :] * jnp.dot(
        mixed, out_weight[...], preferred_element_type=f32
    )
    normal = normalize(after) * (1.0 + modulation_ref[4:5, :]) + modulation_ref[3:4, :]
    inputs = jnp.concatenate(
        [
            (normal[frame * piece : (frame + 1) * piece] + place_ref[frame : frame + 1, :]).astype(bf16)
            for frame in range(frames)
        ],
        axis=0,
    )
    padded = query_ref.shape[1]
    for number, ref in enumerate((query_ref, key_ref, value_ref)):
        ref[:, :width] = jnp.dot(
            inputs, qkv_weight[number], preferred_element_type=f32
        ).astype(bf16)
        ref[:, width:] = jnp.zeros((rows, padded - width), bf16)

    scale = softmax_scale(head_dim)
    step = max(16, min(piece, LANES // frames))
    block = frames * step
    row_at = lax.broadcasted_iota(jnp.int32, (2 * block, block), 0) % step
    column_at = lax.broadcasted_iota(jnp.int32, (2 * block, block), 1) % step
    same = row_at == column_at
    plan = pair_plan(width, head_dim)

    for start in range(0, piece, step):

        def window(ref, tile):
            return jnp.concatenate(
                [
                    ref[
                        frame * piece + start : frame * piece + start + step,
                        tile * LANES : (tile + 2) * LANES,
                    ]
                    for frame in range(frames)
                ],
                axis=0,
            )

        parts = {}
        for tile, lane, _, _ in plan:
            queries = window(query_ref, tile)
            stacked = jnp.concatenate(
                [
                    queries * column_mask(lane, head_dim, bf16),
                    queries * column_mask(lane + head_dim, head_dim, bf16),
                ],
                axis=0,
            )
            scores = lax.dot_general(stacked, window(key_ref, tile), NT, preferred_element_type=f32)
            scores = jnp.where(same, scores * scale, -jnp.inf)
            weights = jnp.exp2(scores - jnp.max(scores, axis=-1, keepdims=True))
            weights = (weights / jnp.sum(weights, axis=-1, keepdims=True)).astype(bf16)
            mixed_pair = jnp.dot(weights, window(value_ref, tile), preferred_element_type=f32)
            joined = mixed_pair[:block] * column_mask(lane, head_dim, f32) + mixed_pair[
                block:
            ] * column_mask(lane + head_dim, head_dim, f32)
            for side in range(2):
                half = joined[:, side * LANES : (side + 1) * LANES]
                parts[tile + side] = parts[tile + side] + half if tile + side in parts else half
        values = jnp.concatenate([parts[tile] for tile in sorted(parts)], axis=1).astype(bf16)
        for frame in range(frames):
            out_refs[frame][start : start + step, :] = values[
                frame * step : (frame + 1) * step, :width
            ]


def temporal(tokens, mixed, spatial_out, temporal_qkv, modulation, places, head_dim):
    frames, groups = len(tokens), len(mixed[0])
    piece = tokens[0].shape[0]
    width, feature_width = spatial_out.shape
    padded = -(-width // LANES) * LANES
    operands = [*tokens, *[part for frame in mixed for part in frame]]
    operands += [spatial_out, temporal_qkv, modulation, places]
    rows = frames * piece
    return pl.pallas_call(
        functools.partial(temporal_kernel, frames=frames, head_dim=head_dim, groups=groups),
        out_shape=[jax.ShapeDtypeStruct((piece, width), bf16) for _ in range(frames)],
        in_specs=vmem_specs(len(operands)),
        out_specs=vmem_specs(frames),
        scratch_shapes=[pltpu.VMEM((rows, padded), bf16) for _ in range(3)],
        cost_estimate=pl.CostEstimate(
            flops=2 * rows * feature_width * width * 8,
            bytes_accessed=rows * feature_width * 8,
            transcendentals=rows * 128 * 8,
        ),
        name="temporal",
    )(*operands)


def output_kernel(slot_ref, after_ref, weight_ref, modulation_ref, *refs, frames, halves):
    parts, out_ref = refs[:-1], refs[-1]
    for frame in range(frames):

        @pl.when(pl.program_id(0) == frame)
        def _():
            mixed = jnp.concatenate([parts[frame * halves + h][...] for h in range(halves)], axis=0)
            out_ref[...] = after_ref[...] + modulation_ref[5:6, :] * jnp.dot(
                mixed, weight_ref[...], preferred_element_type=f32
            )


def output(slot, after, weight, modulation, parts, frames):
    rows, feature_width = after.shape
    piece = rows // frames
    halves = len(parts[0])
    flat = [part for frame in parts for part in frame]

    def whole(array):
        return pl.BlockSpec(array.shape, lambda s, slot_ref: (0,) * array.ndim)

    return pl.pallas_call(
        functools.partial(output_kernel, frames=frames, halves=halves),
        out_shape=jax.ShapeDtypeStruct((rows, feature_width), f32),
        grid_spec=pltpu.PrefetchScalarGridSpec(
            num_scalar_prefetch=1,
            grid=(frames,),
            in_specs=[
                pl.BlockSpec((piece, feature_width), lambda s, slot_ref: (s, 0)),
                whole(weight),
                whole(modulation),
                *[whole(part) for part in flat],
            ],
            out_specs=pl.BlockSpec(
                (piece, feature_width), lambda s, slot_ref: ((s + slot_ref[0]) % frames, 0)
            ),
        ),
        name="block_output",
    )(slot, after, weight, modulation, *flat)


def per_device(
    tokens,
    stale_kv,
    mod_table,
    mod_mix,
    timestep,
    frame_order,
    spatial_qkv,
    spatial_out,
    temporal_qkv,
    temporal_out,
):
    devices = lax.axis_size("patch")
    frames = devices // 4
    slot = lax.axis_index("patch") // 4
    rows, feature_width = tokens.shape
    width = spatial_out.shape[0]
    head_dim = feature_width // HEADS
    piece = rows // frames
    padded = -(-width // LANES) * LANES

    def other_core(device):
        return device ^ 1

    def other_chip(device):
        return device ^ 2

    def ahead(steps):
        return lambda device: (device + 4 * steps) % devices

    near, far = [], []
    for tiles in group_tiles(width, head_dim):
        chunk = jnp.concatenate(
            [stale_kv[:, tile * LANES : (tile + 1) * LANES] for tile in tiles], axis=1
        )
        near.append(permute(chunk, other_chip))
        far.append(permute(near[-1], other_core))
    peer_kv = permute(stale_kv, other_core)

    pieces = [
        lax.dynamic_slice(tokens, ((slot + s) % frames * piece, 0), (piece, feature_width))
        for s in range(frames)
    ]
    there = [pieces[0]] + [permute(pieces[s], ahead(s)) for s in range(1, frames)]

    modulation = mod_table + mod_mix * sinusoid(timestep[0], feature_width)[None, :]
    sources = (slot - jnp.arange(frames)) % frames
    places = sinusoid(frame_order[sources], feature_width)

    tokens_wide = jnp.concatenate(pieces, axis=0).astype(f32)
    spatial_in = (normalize(tokens_wide) * (1.0 + modulation[1]) + modulation[0]).astype(bf16)
    fresh = [
        jnp.dot(spatial_in, spatial_qkv[j], preferred_element_type=f32).astype(bf16) for j in range(3)
    ]
    query = jnp.pad(fresh[0], ((0, 0), (0, padded - width)))
    own_kv = jnp.concatenate([fresh[1], fresh[2]], axis=1)

    carry = None
    local = [[] for _ in range(frames)]
    sent = [[] for _ in range(frames)]
    for number in range(len(PAIR_GROUPS)):
        outs, carry = spatial_group(
            number, query, own_kv, peer_kv, near, far, carry, frames, head_dim, width
        )
        for s in range(frames):
            local[s].append(outs[s])
            sent[s].append(outs[s] if s == 0 else permute(outs[s], ahead(s)))

    half = piece // HALVES
    back = [[] for _ in range(frames)]
    for h in range(HALVES):
        cut = slice(h * half, (h + 1) * half)
        outs = temporal(
            [t[cut] for t in there],
            [[m[cut] for m in frame] for frame in sent],
            spatial_out,
            temporal_qkv,
            modulation,
            places,
            head_dim,
        )
        for s in range(frames):
            back[s].append(outs[s] if s == 0 else permute(outs[s], ahead(-s)))

    spatial_mixed = jnp.concatenate([jnp.concatenate(local[s], axis=1) for s in range(frames)], axis=0)
    after = tokens_wide + modulation[2] * jnp.dot(
        spatial_mixed, spatial_out, preferred_element_type=f32
    )
    return output(
        slot.astype(jnp.int32)[None], after, temporal_out, modulation, back, frames
    )


def solution(mesh):
    return jax.shard_map(
        per_device,
        mesh=mesh,
        in_specs=(
            P(("groups", "patch"), None),
            P(("groups", "patch"), None),
            P(),
            P(),
            P("groups"),
            P("groups"),
            P(),
            P(),
            P(),
            P(),
        ),
        out_specs=P(("groups", "patch"), None),
        check_vma=False,
    )
```

time: 211 us -> 128 us (0.61)
  blocking collectives: 56.9 us -> 0 us
  matrix products: 54.9 us -> 7.95 us
  Pallas kernels: 0 us -> 42.1 us
  starting transfers between devices: 3.11 us -> 27.8 us
  waiting for transfers between devices: 36.3 us -> 13.9 us
  other arithmetic: 18.9 us -> 5.36 us
  local copies, waits for them, and re-layouts: 38.4 us -> 29.4 us
    all_to_all x2 -> x0, blocking collectives: 56.9 us -> none  [the longest x1 35.6 us: per_device(): lax.all_to_all(temporal_in.reshape(devices, piece_rows, feature_width), '...]
    pallas_call x0 -> x6, Pallas kernels: none -> 42.1 us  [the longest x3 21.6 us: spatial_group(): pl.pallas_call(functools.partial(spatial_kernel, group=group, frames=fram...]
    ppermute x2 -> x25, starting transfers between devices: 3.11 us -> 27.8 us  [permute(): lax.ppermute(value, 'patch', [(source, target(source)) for source in rang...]
    sub x2 -> x0, matrix products: 24 us -> none  [softmax_rows(): exp_scores = jnp.exp(scores - row_top)]
    dot_general x6 -> x4, matrix products: 30.9 us -> 7.95 us  [the longest x3 4.5 us: per_device(): jnp.dot(spatial_in, spatial_qkv[j], preferred_element_type=f32).astype(bf16)]
    ppermute x2 -> x25, waiting for transfers between devices: 36.3 us -> 13.9 us  [permute(): lax.ppermute(value, 'patch', [(source, target(source)) for source in rang...]
    another operation x8 -> x0, local copies, waits for them, and re-layouts: 21.1 us -> none  [the longest x1 5.92 us: spatial_attend(): key_heads = key_rows.reshape(-1, head_count, head_dim)]
    slice x1 -> x18, local copies, waits for them, and re-layouts: 0.12 us -> 15.2 us  [the longest x12 8.28 us: per_device(): m[cut]]
  transfers between devices with their start and end apart: 2 -> 25, of which waited for: 1 -> 8; matrix products, arithmetic and copies ran while one was open for 8% -> 31% of each run, Pallas kernels for 0% -> 18%
where the time goes in v1:
time: 128 us
  Pallas kernels  42.1 us (33%)
  local copies, waits for them, and re-layouts  29.4 us (23%)
  starting transfers between devices  27.8 us (22%)
  waiting for transfers between devices  13.9 us (11%)
  matrix products  7.95 us (6%)
  other arithmetic  5.36 us (4%)
  between operations  1.3 us (1%)
    ppermute x25, starting transfers between devices, permute(): lax.ppermute(value, 'patch', [(source, target(source)) for source in rang...  27.8 us
    pallas_call x3, Pallas kernels, spatial_group(): pl.pallas_call(functools.partial(spatial_kernel, group=group, frames=fram...  21.6 us
    pallas_call x2, Pallas kernels, temporal(): pl.pallas_call(functools.partial(temporal_kernel, frames=frames, head_dim...  15.3 us
    ppermute x25, waiting for transfers between devices, permute(): lax.ppermute(value, 'patch', [(source, target(source)) for source in rang...  13.9 us
    unnamed x59, local copies, waits for them, and re-layouts  9.56 us
    slice x12, local copies, waits for them, and re-layouts, per_device(): m[cut]  8.28 us
    pallas_call x1, Pallas kernels, output(): pl.pallas_call(functools.partial(output_kernel, frames=frames, halves=hal...  5.22 us
    dot_general x3, matrix products, per_device(): jnp.dot(spatial_in, spatial_qkv[j], preferred_element_type=f32).astype(bf16)  4.5 us
  transfers between devices with their start and end apart: 25, of which 8 were waited for; matrix products, arithmetic and copies ran while one was open for 31% of the time, Pallas kernels for 18%

profile of v1, /device:TPU:0, one launch (start us, length us, event | category | flops | bytes accessed | tf_op | source)
XLA Modules:
  0.0 127.8 jit_solution(3622151349285643394)
XLA Ops:
  0.5 1.2 fusion.52
  1.7 1.0 pad_maximum_fusion.2
  2.7 2.5 %collective-permute-start.1 = (bf16[512,768]{1,0:T(8,128)(2,1)}, bf16[512,768]{1,0:T(8,128)(2,1)}, u32[]{:S(2)}, u32[]{:S(2)}) collective-permute-start(bf16[512,768]{1,0:T(8,128)(2,1)} %pad_maximum_fusion.2), channel_id=1, source_target_pairs={{0,2},{1,3},{2,0},{3,1},{4,6},{5,7},{6,4},{7,5},{8,10},{9,11},{10,... | collective-permute-start | bytes 2359304 | tf_op jit(solution)/shard_map/ppermute | solution.py:25
  5.2 1.7 %fusion.51 = (bf16[512,128]{1,0:T(8,128)(2,1)}, bf16[512,128]{1,0:T(8,128)(2,1)S(1)}, bf16[512,128]{1,0:T(8,128)(2,1)S(1)}) fusion(bf16[512,1152]{1,0:T(8,128)(2,1)} %param.11), kind=kLoop, calls=%fused_computation.78 | loop fusion | bytes 786432 | tf_op jit(solution)/shard_map/slice | solution.py:408
  6.9 0.8 pad_maximum_fusion.3
  7.8 4.2 %collective-permute-start.9 = (bf16[128,1152]{1,0:T(8,128)(2,1)S(1)}, bf16[128,1152]{1,0:T(8,128)(2,1)}, u32[]{:S(2)}, u32[]{:S(2)}) collective-permute-start(bf16[128,1152]{1,0:T(8,128)(2,1)S(1)} %get-tuple-element.61), channel_id=1, source_target_pairs={{0,12},{1,13},{2,14},{3,15},{4,0},{5,1},{6,2},{7,3},{8,4},{9,5},{1... | collective-permute-start | bytes 884744 | tf_op jit(solution)/shard_map/ppermute | solution.py:25
  14.4 1.8 %fusion.18 = bf16[512,576]{0,1:T(8,128)(2,1)} fusion(bf16[512,1152]{1,0:T(8,128)(2,1)S(1)} %fusion.5, bf16[3,1152,576]{1,2,0:T(8,128)(2,1)S(1)} %copy-done.15), kind=kOutput, calls=%fused_computation.21 | convolution fusion | flops 679772160 | bytes 3096576 | tf_op jit(solution)/shard_map/dot_general | solution.py:427
  16.2 1.0 fusion.21
  17.2 1.8 %fusion.15 = bf16[512,576]{0,1:T(8,128)(2,1)} fusion(bf16[512,1152]{1,0:T(8,128)(2,1)S(1)} %fusion.5, bf16[3,1152,576]{1,2,0:T(8,128)(2,1)S(1)} %copy-done.15), kind=kOutput, calls=%fused_computation.20 | convolution fusion | flops 679772160 | bytes 3096576 | tf_op jit(solution)/shard_map/dot_general | solution.py:427
  19.0 0.8 constant_dynamic-slice_fusion
  20.5 0.7 pad_maximum_fusion.4.refs_19_
  21.2 1.4 %copy.22 = bf16[512,576]{1,0:T(8,128)(2,1)S(1)} copy(bf16[512,576]{0,1:T(8,128)(2,1)} %fusion.18) | data formatting | bytes 1179648 | tf_op jit(solution)/shard_map/convert_element_type | solution.py:427
  22.9 1.4 %copy.21 = bf16[512,576]{1,0:T(8,128)(2,1)S(1)} copy(bf16[512,576]{0,1:T(8,128)(2,1)} %fusion.15) | data formatting | bytes 1179648 | tf_op jit(solution)/shard_map/convert_element_type | solution.py:427
  24.2 6.6 %copy.24.refs_17_ = bf16[3,1152,576]{2,1,0:T(8,128)(2,1)} copy(bf16[3,1152,576]{1,2,0:T(8,128)(2,1)} %param.18) | data formatting | bytes 7962624 | tf_op args[8]
  30.8 0.9 pad.4.refs_0_
  31.7 1.4 %pad_maximum_fusion.1.refs_1_ = bf16[512,1152]{1,0:T(8,128)(2,1)} fusion(bf16[512,576]{1,0:T(8,128)(2,1)S(1)} %copy.23, bf16[512,576]{1,0:T(8,128)(2,1)S(1)} %copy.22), kind=kLoop, calls=%fused_computation.24 | loop fusion | flops 2359296 | bytes 2359296 | tf_op jit(solution)/shard_map/concatenate | solution.py:430
  33.1 1.5 %collective-permute-start.5 = (bf16[512,128]{1,0:T(8,128)(2,1)S(1)}, bf16[512,128]{1,0:T(8,128)(2,1)S(1)}, u32[]{:S(2)}, u32[]{:S(2)}) collective-permute-start(bf16[512,128]{1,0:T(8,128)(2,1)S(1)} %copy-done.3), channel_id=1, source_target_pairs={{0,2},{1,3},{2,0},{3,1},{4,6},{5,7},{6,4},{7,5},{8,10},{9,11},{10,... | collective-permute-start | bytes 393224 | tf_op jit(solution)/shard_map/ppermute | solution.py:25
  34.6 1.8 %fusion.53 = (bf16[64,1152]{1,0:T(8,128)(2,1)}, bf16[64,1152]{1,0:T(8,128)(2,1)}) fusion(bf16[128,1152]{1,0:T(8,128)(2,1)} %collective-permute-done.9), kind=kLoop, calls=%fused_computation.80 | loop fusion | bytes 589824 | tf_op jit(solution)/shard_map/slice | solution.py:448
  36.4 1.8 %collective-permute-done.5.refs_5_ = bf16[512,128]{1,0:T(8,128)(2,1)S(1)} collective-permute-done((bf16[512,128]{1,0:T(8,128)(2,1)S(1)}, bf16[512,128]{1,0:T(8,128)(2,1)S(1)}, u32[]{:S(2)}, u32[]{:S(2)}) %collective-permute-start.5) | collective-permute-done | bytes 131104 | tf_op jit(solution)/shard_map/ppermute | solution.py:25
  38.2 0.9 collective-permute-start.7
  39.7 0.7 fusion.54
  40.4 7.3 %collective-permute-done.7 = bf16[128,1152]{1,0:T(8,128)(2,1)S(1)} collective-permute-done((bf16[128,1152]{1,0:T(8,128)(2,1)S(1)}, bf16[128,1152]{1,0:T(8,128)(2,1)S(1)}, u32[]{:S(2)}, u32[]{:S(2)}) %collective-permute-start.7) | collective-permute-done | bytes 294944 | tf_op jit(solution)/shard_map/ppermute | solution.py:25
  47.7 0.7 fusion.55
  48.4 0.9 copy-done.17
  49.3 8.9 %spatial_0.1 = (bf16[128,256]{1,0:T(8,128)(2,1)}, bf16[128,256]{1,0:T(8,128)(2,1)}, bf16[128,256]{1,0:T(8,128)(2,1)}, bf16[128,256]{1,0:T(8,128)(2,1)}, bf16[512,128]{1,0:T(8,128)(2,1)}) custom-call(bf16[512,640]{1,0:T(8,128)(2,1)} %pad.4.refs_0_, bf16[512,1152]{1,0:T(8,128)(2,1)} %pad_maximum_fusion.1.refs_1_, ...), custom_call_target="tpu_custom_call" | custom-call | flops 4294967296 | bytes 2097152 | tf_op jit(solution)/shard_map/spatial_0/pallas_call | solution.py:201
  58.2 0.7 copy-done.18
  58.9 6.2 %spatial_1.1 = (bf16[128,128]{1,0:T(8,128)(2,1)}, bf16[128,128]{1,0:T(8,128)(2,1)}, bf16[128,128]{1,0:T(8,128)(2,1)}, bf16[128,128]{1,0:T(8,128)(2,1)}, bf16[512,128]{1,0:T(8,128)(2,1)}) custom-call(bf16[512,640]{1,0:T(8,128)(2,1)} %pad.4.refs_0_, bf16[512,1152]{1,0:T(8,128)(2,1)} %pad_maximum_fusion.1.refs_1_, ...), custom_call_target="tpu_custom_call" | custom-call | flops 2147483648 | bytes 2097152 | tf_op jit(solution)/shard_map/spatial_1/pallas_call | solution.py:201
  65.8 6.5 %spatial_2.1 = (bf16[128,192]{1,0:T(8,128)(2,1)}, bf16[128,192]{1,0:T(8,128)(2,1)}, bf16[128,192]{1,0:T(8,128)(2,1)}, bf16[128,192]{1,0:T(8,128)(2,1)}) custom-call(bf16[512,640]{1,0:T(8,128)(2,1)} %pad.4.refs_0_, bf16[512,1152]{1,0:T(8,128)(2,1)} %pad_maximum_fusion.1.refs_1_, bf16[512,1152]{1,0:T(8,128)(2,1)} %collective-permute-done.refs_2_, ...), custom_call_target="tpu_custom_call" | custom-call | flops 2147483648 | bytes 2097152 | tf_op jit(solution)/shard_map/spatial_2/pallas_call | solution.py:201
  72.9 2.0 %collective-permute-start.12 = (bf16[128,192]{1,0:T(8,128)(2,1)}, bf16[128,192]{1,0:T(8,128)(2,1)S(1)}, u32[]{:S(2)}, u32[]{:S(2)}) collective-permute-start(bf16[128,192]{1,0:T(8,128)(2,1)} %get-tuple-element.34), channel_id=1, source_target_pairs={{0,4},{1,5},{2,6},{3,7},{4,8},{5,9},{6,10},{7,11},{8,12},{9,13},{1... | collective-permute-start | bytes 147464 | tf_op jit(solution)/shard_map/ppermute | solution.py:25
  74.9 1.4 %fusion.62 = (bf16[64,192]{1,0:T(8,128)(2,1)}, bf16[64,192]{1,0:T(8,128)(2,1)}) fusion(bf16[128,192]{1,0:T(8,128)(2,1)} %get-tuple-element.31), kind=kLoop, calls=%fused_computation.89 | loop fusion | bytes 98304 | tf_op jit(solution)/shard_map/slice | solution.py:449
  76.3 1.9 %collective-permute-start.17 = (bf16[128,128]{1,0:T(8,128)(2,1)S(1)}, bf16[128,128]{1,0:T(8,128)(2,1)S(1)}, u32[]{:S(2)}, u32[]{:S(2)}) collective-permute-start(bf16[128,128]{1,0:T(8,128)(2,1)S(1)} %copy-done.28), channel_id=1, source_target_pairs={{0,12},{1,13},{2,14},{3,15},{4,0},{5,1},{6,2},{7,3},{8,4},{9,5},{1... | collective-permute-start | bytes 98312 | tf_op jit(solution)/shard_map/ppermute | solution.py:25
  78.2 0.7 collective-permute-start.14
  80.7 1.3 %collective-permute-start.11 = (bf16[128,128]{1,0:T(8,128)(2,1)S(1)}, bf16[128,128]{1,0:T(8,128)(2,1)S(1)}, u32[]{:S(2)}, u32[]{:S(2)}) collective-permute-start(bf16[128,128]{1,0:T(8,128)(2,1)S(1)} %copy-done.26), channel_id=1, source_target_pairs={{0,4},{1,5},{2,6},{3,7},{4,8},{5,9},{6,10},{7,11},{8,12},{9,13},{1... | collective-permute-start | bytes 98312 | tf_op jit(solution)/shard_map/ppermute | solution.py:25
  82.6 0.7 collective-permute-done.14
  83.4 1.8 %collective-permute-start.16 = (bf16[128,256]{1,0:T(8,128)(2,1)S(1)}, bf16[128,256]{1,0:T(8,128)(2,1)S(1)}, u32[]{:S(2)}, u32[]{:S(2)}) collective-permute-start(bf16[128,256]{1,0:T(8,128)(2,1)S(1)} %copy-done.23), channel_id=1, source_target_pairs={{0,12},{1,13},{2,14},{3,15},{4,0},{5,1},{6,2},{7,3},{8,4},{9,5},{1... | collective-permute-start | bytes 196616 | tf_op jit(solution)/shard_map/ppermute | solution.py:25
  85.8 0.9 collective-permute-done.11
  87.6 2.1 %collective-permute-start.10 = (bf16[128,256]{1,0:T(8,128)(2,1)S(1)}, bf16[128,256]{1,0:T(8,128)(2,1)S(1)}, u32[]{:S(2)}, u32[]{:S(2)}) collective-permute-start(bf16[128,256]{1,0:T(8,128)(2,1)S(1)} %copy-done.21), channel_id=1, source_target_pairs={{0,4},{1,5},{2,6},{3,7},{4,8},{5,9},{6,10},{7,11},{8,12},{9,13},{1... | collective-permute-start | bytes 196616 | tf_op jit(solution)/shard_map/ppermute | solution.py:25
  92.8 0.8 collective-permute-done.10
  94.3 7.6 %temporal.3 = (bf16[64,576]{1,0:T(8,128)(2,1)}, bf16[64,576]{1,0:T(8,128)(2,1)}, bf16[64,576]{1,0:T(8,128)(2,1)}, bf16[64,576]{1,0:T(8,128)(2,1)}) custom-call(bf16[64,1152]{1,0:T(8,128)(2,1)} %get-tuple-element.52.refs_0_, bf16[64,1152]{1,0:T(8,128)(2,1)} %get-tuple-element.67.refs_1_, bf16[64,1152]{1,0:T(8,128)(2,1)} %get-tuple-element.65.refs_2_, ...), custom_call_target="tpu_custom_call" | custom-call | flops 2717908992 | bytes 2359296 | tf_op jit(solution)/shard_map/temporal/pallas_call | solution.py:319
  101.9 1.0 collective-permute-start.20
  102.9 0.9 collective-permute-start.22
  103.7 1.1 collective-permute-start.24
  104.8 7.7 %temporal.2 = (bf16[64,576]{1,0:T(8,128)(2,1)}, bf16[64,576]{1,0:T(8,128)(2,1)}, bf16[64,576]{1,0:T(8,128)(2,1)}, bf16[64,576]{1,0:T(8,128)(2,1)}) custom-call(bf16[64,1152]{1,0:T(8,128)(2,1)} %get-tuple-element.53.refs_0_, bf16[64,1152]{1,0:T(8,128)(2,1)} %get-tuple-element.68.refs_1_, bf16[64,1152]{1,0:T(8,128)(2,1)} %get-tuple-element.66.refs_2_, ...), custom_call_target="tpu_custom_call" | custom-call | flops 2717908992 | bytes 2359296 | tf_op jit(solution)/shard_map/temporal/pallas_call | solution.py:319
  112.5 2.8 %collective-permute-start.19 = (bf16[64,576]{1,0:T(8,128)(2,1)}, bf16[64,576]{1,0:T(8,128)(2,1)S(1)}, u32[]{:S(2)}, u32[]{:S(2)}) collective-permute-start(bf16[64,576]{1,0:T(8,128)(2,1)} %get-tuple-element.43), channel_id=1, source_target_pairs={{0,12},{1,13},{2,14},{3,15},{4,0},{5,1},{6,2},{7,3},{8,4},{9,5},{1... | collective-permute-start | bytes 221192 | tf_op jit(solution)/shard_map/ppermute | solution.py:25
  115.5 1.1 collective-permute-start.23
  116.6 3.4 %convert_add_fusion.after_ref = f32[512,1152]{1,0:T(8,128)} fusion(bf16[576,1152]{1,0:T(8,128)(2,1)S(1)} %copy-done.16, f32[1152]{0:T(1024)S(1)} %get-tuple-element.51, bf16[128,192]{1,0:T(8,128)(2,1)} %get-tuple-element.40, bf16[128,128]{1,0:T(8,128)(2,1)} %get-tuple-element.39, bf16[128,256]{1,0:T(8,128)(2,1)S(1)} %copy-done.23, ...), kind=kOutput, calls=%fused_computation.1 | convolution fusion | flops 692453376 | bytes 5460480 | tf_op jit(solution)/shard_map/dot_general | solution.py:460
  120.8 1.2 collective-permute-done.23.refs_6_
  122.6 5.2 %block_output.1 = f32[512,1152]{1,0:T(8,128)} custom-call(s32[1]{0:T(128)} %bitcast.slot_ref, f32[512,1152]{1,0:T(8,128)} %convert_add_fusion.after_ref, bf16[576,1152]{1,0:T(8,128)(2,1)} %weight_ref.1, f32[6,1152]{1,0:T(8,128)} %copy-done.2, bf16[64,576]{1,0:T(8,128)(2,1)} %get-tuple-element.41.refs_0_, bf16[64,576]{1,0:T(8,128)(2,1)} %get-tuple-element.42.refs_1_, ...), custom_call_target="tpu_custom_call" | custom-call | tf_op jit(solution)/shard_map/block_output/pallas_call | solution.py:355
  (113 shorter events, 14.2 us)
Async XLA Ops:
  0.0 19.7 %copy-start = (s32[4]{0:T(128)S(1)}, s32[4]{0:T(128)}, u32[]{:S(2)}) copy-start(s32[4]{0:T(128)} %param.15) | copy-start | bytes 52
  0.0 48.4 %collective-permute-start = (bf16[512,1152]{1,0:T(8,128)(2,1)}, bf16[512,1152]{1,0:T(8,128)(2,1)}, u32[]{:S(2)}, u32[]{:S(2)}) collective-permute-start(bf16[512,1152]{1,0:T(8,128)(2,1)} %param.11), channel_id=1, source_target_pairs={{0,1},{1,0},{2,3},{3,2},{4,5},{5,4},{6,7},{7,6},{8,9},{9,8},{10,11... | collective-permute-start | bytes 3538952 | tf_op jit(solution)/shard_map/ppermute | solution.py:25
  1.7 6.0 %copy-start.1 = (bf16[512,1152]{1,0:T(8,128)(2,1)S(1)}, bf16[512,1152]{1,0:T(8,128)(2,1)}, u32[]{:S(2)}) copy-start(bf16[512,1152]{1,0:T(8,128)(2,1)} %param.10) | copy-start | bytes 3538948
  2.7 36.9 %collective-permute-start.1 = (bf16[512,768]{1,0:T(8,128)(2,1)}, bf16[512,768]{1,0:T(8,128)(2,1)}, u32[]{:S(2)}, u32[]{:S(2)}) collective-permute-start(bf16[512,768]{1,0:T(8,128)(2,1)} %pad_maximum_fusion.2), channel_id=1, source_target_pairs={{0,2},{1,3},{2,0},{3,1},{4,6},{5,7},{6,4},{7,5},{8,10},{9,11},{10,... | collective-permute-start | bytes 2359304 | tf_op jit(solution)/shard_map/ppermute | solution.py:25
  7.7 31.4 %collective-permute-start.3 = (bf16[512,256]{1,0:T(8,128)(2,1)}, bf16[512,256]{1,0:T(8,128)(2,1)}, u32[]{:S(2)}, u32[]{:S(2)}) collective-permute-start(bf16[512,256]{1,0:T(8,128)(2,1)} %pad_maximum_fusion.3), channel_id=1, source_target_pairs={{0,2},{1,3},{2,0},{3,1},{4,6},{5,7},{6,4},{7,5},{8,10},{9,11},{10,... | collective-permute-start | bytes 786440 | tf_op jit(solution)/shard_map/ppermute | solution.py:25
  7.8 6.0 %copy-start.12 = (f32[6,1152]{1,0:T(8,128)S(1)}, f32[6,1152]{1,0:T(8,128)}, u32[]{:S(2)}) copy-start(f32[6,1152]{1,0:T(8,128)} %param.12) | copy-start | bytes 82948
  7.8 6.0 %copy-start.13 = (f32[6,1152]{1,0:T(8,128)S(1)}, f32[6,1152]{1,0:T(8,128)}, u32[]{:S(2)}) copy-start(f32[6,1152]{1,0:T(8,128)} %param.13) | copy-start | bytes 82948
  7.8 25.3 %collective-permute-start.9 = (bf16[128,1152]{1,0:T(8,128)(2,1)S(1)}, bf16[128,1152]{1,0:T(8,128)(2,1)}, u32[]{:S(2)}, u32[]{:S(2)}) collective-permute-start(bf16[128,1152]{1,0:T(8,128)(2,1)S(1)} %get-tuple-element.61), channel_id=1, source_target_pairs={{0,12},{1,13},{2,14},{3,15},{4,0},{5,1},{6,2},{7,3},{8,4},{9,5},{1... | collective-permute-start | bytes 884744 | tf_op jit(solution)/shard_map/ppermute | solution.py:25
  12.0 27.1 %collective-permute-start.8 = (bf16[128,1152]{1,0:T(8,128)(2,1)S(1)}, bf16[128,1152]{1,0:T(8,128)(2,1)S(1)}, u32[]{:S(2)}, u32[]{:S(2)}) collective-permute-start(bf16[128,1152]{1,0:T(8,128)(2,1)S(1)} %get-tuple-element.62), channel_id=1, source_target_pairs={{0,8},{1,9},{2,10},{3,11},{4,12},{5,13},{6,14},{7,15},{8,0},{9,1},... | collective-permute-start | bytes 884744 | tf_op jit(solution)/shard_map/ppermute | solution.py:25
  12.0 2.4 %copy-start.15 = (bf16[3,1152,576]{1,2,0:T(8,128)(2,1)S(1)}, bf16[3,1152,576]{1,2,0:T(8,128)(2,1)}, u32[]{:S(2)}) copy-start(bf16[3,1152,576]{1,2,0:T(8,128)(2,1)} %param.16) | copy-start | bytes 11943940
  13.8 2.4 %copy-start.2 = (f32[6,1152]{1,0:T(8,128)}, f32[6,1152]{1,0:T(8,128)S(1)}, u32[]{:S(2)}) copy-start(f32[6,1152]{1,0:T(8,128)S(1)} %multiply_add_fusion.refs_18_.modulation_ref) | copy-start | bytes 82948
  33.1 5.1 %collective-permute-start.5 = (bf16[512,128]{1,0:T(8,128)(2,1)S(1)}, bf16[512,128]{1,0:T(8,128)(2,1)S(1)}, u32[]{:S(2)}, u32[]{:S(2)}) collective-permute-start(bf16[512,128]{1,0:T(8,128)(2,1)S(1)} %copy-done.3), channel_id=1, source_target_pairs={{0,2},{1,3},{2,0},{3,1},{4,6},{5,7},{6,4},{7,5},{8,10},{9,11},{10,... | collective-permute-start | bytes 393224 | tf_op jit(solution)/shard_map/ppermute | solution.py:25
  38.2 20.0 %copy-start.19 = (bf16[512,128]{1,0:T(8,128)(2,1)}, bf16[512,128]{1,0:T(8,128)(2,1)S(1)}, u32[]{:S(2)}) copy-start(bf16[512,128]{1,0:T(8,128)(2,1)S(1)} %collective-permute-done.5.refs_5_) | copy-start | bytes 393220
  38.2 9.5 %collective-permute-start.7 = (bf16[128,1152]{1,0:T(8,128)(2,1)S(1)}, bf16[128,1152]{1,0:T(8,128)(2,1)S(1)}, u32[]{:S(2)}, u32[]{:S(2)}) collective-permute-start(bf16[128,1152]{1,0:T(8,128)(2,1)S(1)} %get-tuple-element.60), channel_id=1, source_target_pairs={{0,4},{1,5},{2,6},{3,7},{4,8},{5,9},{6,10},{7,11},{8,12},{9,13},{1... | collective-permute-start | bytes 884744 | tf_op jit(solution)/shard_map/ppermute | solution.py:25
  39.1 26.0 %collective-permute-start.6 = (bf16[512,128]{1,0:T(8,128)(2,1)S(1)}, bf16[512,128]{1,0:T(8,128)(2,1)S(1)}, u32[]{:S(2)}, u32[]{:S(2)}) collective-permute-start(bf16[512,128]{1,0:T(8,128)(2,1)S(1)} %collective-permute-done.5.refs_5_), channel_id=1, source_target_pairs={{0,1},{1,0},{2,3},{3,2},{4,5},{5,4},{6,7},{7,6},{8,9},{9,8},{10,11... | collective-permute-start | bytes 393224 | tf_op jit(solution)/shard_map/ppermute | solution.py:25
  39.1 19.1 %collective-permute-start.4 = (bf16[512,256]{1,0:T(8,128)(2,1)}, bf16[512,256]{1,0:T(8,128)(2,1)S(1)}, u32[]{:S(2)}, u32[]{:S(2)}) collective-permute-start(bf16[512,256]{1,0:T(8,128)(2,1)} %collective-permute-done.3.refs_4_), channel_id=1, source_target_pairs={{0,1},{1,0},{2,3},{3,2},{4,5},{5,4},{6,7},{7,6},{8,9},{9,8},{10,11... | collective-permute-start | bytes 786440 | tf_op jit(solution)/shard_map/ppermute | solution.py:25
  39.6 8.8 %collective-permute-start.2 = (bf16[512,768]{1,0:T(8,128)(2,1)}, bf16[512,768]{1,0:T(8,128)(2,1)S(1)}, u32[]{:S(2)}, u32[]{:S(2)}) collective-permute-start(bf16[512,768]{1,0:T(8,128)(2,1)} %collective-permute-done.1.refs_3_), channel_id=1, source_target_pairs={{0,1},{1,0},{2,3},{3,2},{4,5},{5,4},{6,7},{7,6},{8,9},{9,8},{10,11... | collective-permute-start | bytes 2359304 | tf_op jit(solution)/shard_map/ppermute | solution.py:25
  65.8 10.5 %copy-start.28 = (bf16[128,128]{1,0:T(8,128)(2,1)S(1)}, bf16[128,128]{1,0:T(8,128)(2,1)}, u32[]{:S(2)}) copy-start(bf16[128,128]{1,0:T(8,128)(2,1)} %get-tuple-element.39) | copy-start | bytes 98308
  65.8 12.4 %copy-start.27 = (bf16[128,128]{1,0:T(8,128)(2,1)S(1)}, bf16[128,128]{1,0:T(8,128)(2,1)}, u32[]{:S(2)}) copy-start(bf16[128,128]{1,0:T(8,128)(2,1)} %get-tuple-element.36) | copy-start | bytes 98308
  65.8 13.1 %copy-start.10 = (bf16[128,256]{1,0:T(8,128)(2,1)S(1)}, bf16[128,256]{1,0:T(8,128)(2,1)}, u32[]{:S(2)}) copy-start(bf16[128,256]{1,0:T(8,128)(2,1)} %get-tuple-element.27) | copy-start | bytes 196612
  65.8 13.8 %copy-start.14 = (bf16[128,128]{1,0:T(8,128)(2,1)S(1)}, bf16[128,128]{1,0:T(8,128)(2,1)}, u32[]{:S(2)}) copy-start(bf16[128,128]{1,0:T(8,128)(2,1)} %get-tuple-element.29) | copy-start | bytes 98308
  65.8 14.9 %copy-start.26 = (bf16[128,128]{1,0:T(8,128)(2,1)S(1)}, bf16[128,128]{1,0:T(8,128)(2,1)}, u32[]{:S(2)}) copy-start(bf16[128,128]{1,0:T(8,128)(2,1)} %get-tuple-element.33) | copy-start | bytes 98308
  65.8 17.5 %copy-start.23 = (bf16[128,256]{1,0:T(8,128)(2,1)S(1)}, bf16[128,256]{1,0:T(8,128)(2,1)}, u32[]{:S(2)}) copy-start(bf16[128,256]{1,0:T(8,128)(2,1)} %get-tuple-element.38) | copy-start | bytes 196612
  65.8 20.8 %copy-start.22 = (bf16[128,256]{1,0:T(8,128)(2,1)S(1)}, bf16[128,256]{1,0:T(8,128)(2,1)}, u32[]{:S(2)}) copy-start(bf16[128,256]{1,0:T(8,128)(2,1)} %get-tuple-element.35) | copy-start | bytes 196612
  65.8 21.7 %copy-start.21 = (bf16[128,256]{1,0:T(8,128)(2,1)S(1)}, bf16[128,256]{1,0:T(8,128)(2,1)}, u32[]{:S(2)}) copy-start(bf16[128,256]{1,0:T(8,128)(2,1)} %get-tuple-element.32) | copy-start | bytes 196612
  72.4 15.2 %collective-permute-start.18 = (bf16[128,192]{1,0:T(8,128)(2,1)}, bf16[128,192]{1,0:T(8,128)(2,1)S(1)}, u32[]{:S(2)}, u32[]{:S(2)}) collective-permute-start(bf16[128,192]{1,0:T(8,128)(2,1)} %get-tuple-element.40), channel_id=1, source_target_pairs={{0,12},{1,13},{2,14},{3,15},{4,0},{5,1},{6,2},{7,3},{8,4},{9,5},{1... | collective-permute-start | bytes 147464 | tf_op jit(solution)/shard_map/ppermute | solution.py:25
  72.6 17.7 %collective-permute-start.15 = (bf16[128,192]{1,0:T(8,128)(2,1)}, bf16[128,192]{1,0:T(8,128)(2,1)S(1)}, u32[]{:S(2)}, u32[]{:S(2)}) collective-permute-start(bf16[128,192]{1,0:T(8,128)(2,1)} %get-tuple-element.37), channel_id=1, source_target_pairs={{0,8},{1,9},{2,10},{3,11},{4,12},{5,13},{6,14},{7,15},{8,0},{9,1},... | collective-permute-start | bytes 147464 | tf_op jit(solution)/shard_map/ppermute | solution.py:25
  72.9 18.0 %collective-permute-start.12 = (bf16[128,192]{1,0:T(8,128)(2,1)}, bf16[128,192]{1,0:T(8,128)(2,1)S(1)}, u32[]{:S(2)}, u32[]{:S(2)}) collective-permute-start(bf16[128,192]{1,0:T(8,128)(2,1)} %get-tuple-element.34), channel_id=1, source_target_pairs={{0,4},{1,5},{2,6},{3,7},{4,8},{5,9},{6,10},{7,11},{8,12},{9,13},{1... | collective-permute-start | bytes 147464 | tf_op jit(solution)/shard_map/ppermute | solution.py:25
  76.3 4.4 %collective-permute-start.17 = (bf16[128,128]{1,0:T(8,128)(2,1)S(1)}, bf16[128,128]{1,0:T(8,128)(2,1)S(1)}, u32[]{:S(2)}, u32[]{:S(2)}) collective-permute-start(bf16[128,128]{1,0:T(8,128)(2,1)S(1)} %copy-done.28), channel_id=1, source_target_pairs={{0,12},{1,13},{2,14},{3,15},{4,0},{5,1},{6,2},{7,3},{8,4},{9,5},{1... | collective-permute-start | bytes 98312 | tf_op jit(solution)/shard_map/ppermute | solution.py:25
  78.2 5.2 %collective-permute-start.14 = (bf16[128,128]{1,0:T(8,128)(2,1)S(1)}, bf16[128,128]{1,0:T(8,128)(2,1)S(1)}, u32[]{:S(2)}, u32[]{:S(2)}) collective-permute-start(bf16[128,128]{1,0:T(8,128)(2,1)S(1)} %copy-done.27), channel_id=1, source_target_pairs={{0,8},{1,9},{2,10},{3,11},{4,12},{5,13},{6,14},{7,15},{8,0},{9,1},... | collective-permute-start | bytes 98312 | tf_op jit(solution)/shard_map/ppermute | solution.py:25
  80.7 6.0 %collective-permute-start.11 = (bf16[128,128]{1,0:T(8,128)(2,1)S(1)}, bf16[128,128]{1,0:T(8,128)(2,1)S(1)}, u32[]{:S(2)}, u32[]{:S(2)}) collective-permute-start(bf16[128,128]{1,0:T(8,128)(2,1)S(1)} %copy-done.26), channel_id=1, source_target_pairs={{0,4},{1,5},{2,6},{3,7},{4,8},{5,9},{6,10},{7,11},{8,12},{9,13},{1... | collective-permute-start | bytes 98312 | tf_op jit(solution)/shard_map/ppermute | solution.py:25
  83.4 8.2 %collective-permute-start.16 = (bf16[128,256]{1,0:T(8,128)(2,1)S(1)}, bf16[128,256]{1,0:T(8,128)(2,1)S(1)}, u32[]{:S(2)}, u32[]{:S(2)}) collective-permute-start(bf16[128,256]{1,0:T(8,128)(2,1)S(1)} %copy-done.23), channel_id=1, source_target_pairs={{0,12},{1,13},{2,14},{3,15},{4,0},{5,1},{6,2},{7,3},{8,4},{9,5},{1... | collective-permute-start | bytes 196616 | tf_op jit(solution)/shard_map/ppermute | solution.py:25
  86.7 5.5 %collective-permute-start.13 = (bf16[128,256]{1,0:T(8,128)(2,1)S(1)}, bf16[128,256]{1,0:T(8,128)(2,1)S(1)}, u32[]{:S(2)}, u32[]{:S(2)}) collective-permute-start(bf16[128,256]{1,0:T(8,128)(2,1)S(1)} %copy-done.22), channel_id=1, source_target_pairs={{0,8},{1,9},{2,10},{3,11},{4,12},{5,13},{6,14},{7,15},{8,0},{9,1},... | collective-permute-start | bytes 196616 | tf_op jit(solution)/shard_map/ppermute | solution.py:25
  87.6 6.1 %collective-permute-start.10 = (bf16[128,256]{1,0:T(8,128)(2,1)S(1)}, bf16[128,256]{1,0:T(8,128)(2,1)S(1)}, u32[]{:S(2)}, u32[]{:S(2)}) collective-permute-start(bf16[128,256]{1,0:T(8,128)(2,1)S(1)} %copy-done.21), channel_id=1, source_target_pairs={{0,4},{1,5},{2,6},{3,7},{4,8},{5,9},{6,10},{7,11},{8,12},{9,13},{1... | collective-permute-start | bytes 196616 | tf_op jit(solution)/shard_map/ppermute | solution.py:25
  101.9 13.6 %collective-permute-start.20 = (bf16[64,576]{1,0:T(8,128)(2,1)}, bf16[64,576]{1,0:T(8,128)(2,1)S(1)}, u32[]{:S(2)}, u32[]{:S(2)}) collective-permute-start(bf16[64,576]{1,0:T(8,128)(2,1)} %get-tuple-element.44), channel_id=1, source_target_pairs={{0,12},{1,13},{2,14},{3,15},{4,0},{5,1},{6,2},{7,3},{8,4},{9,5},{1... | collective-permute-start | bytes 221192 | tf_op jit(solution)/shard_map/ppermute | solution.py:25
  102.9 17.2 %collective-permute-start.22 = (bf16[64,576]{1,0:T(8,128)(2,1)}, bf16[64,576]{1,0:T(8,128)(2,1)S(1)}, u32[]{:S(2)}, u32[]{:S(2)}) collective-permute-start(bf16[64,576]{1,0:T(8,128)(2,1)} %get-tuple-element.46), channel_id=1, source_target_pairs={{0,8},{1,9},{2,10},{3,11},{4,12},{5,13},{6,14},{7,15},{8,0},{9,1},... | collective-permute-start | bytes 221192 | tf_op jit(solution)/shard_map/ppermute | solution.py:25
  103.7 16.4 %collective-permute-start.24 = (bf16[64,576]{1,0:T(8,128)(2,1)}, bf16[64,576]{1,0:T(8,128)(2,1)S(1)}, u32[]{:S(2)}, u32[]{:S(2)}) collective-permute-start(bf16[64,576]{1,0:T(8,128)(2,1)} %get-tuple-element.48), channel_id=1, source_target_pairs={{0,4},{1,5},{2,6},{3,7},{4,8},{5,9},{6,10},{7,11},{8,12},{9,13},{1... | collective-permute-start | bytes 221192 | tf_op jit(solution)/shard_map/ppermute | solution.py:25
  104.8 11.8 %copy-start.11 = (bf16[128,192]{1,0:T(8,128)(2,1)S(1)}, bf16[128,192]{1,0:T(8,128)(2,1)}, u32[]{:S(2)}) copy-start(bf16[128,192]{1,0:T(8,128)(2,1)} %get-tuple-element.31) | copy-start | bytes 147460
  104.8 11.8 %copy-start.16 = (bf16[576,1152]{1,0:T(8,128)(2,1)S(1)}, bf16[576,1152]{1,0:T(8,128)(2,1)}, u32[]{:S(2)}) copy-start(bf16[576,1152]{1,0:T(8,128)(2,1)} %refs_16_.3) | copy-start | bytes 3981316
  104.8 11.8 %copy-start.24 = (bf16[128,192]{1,0:T(8,128)(2,1)S(1)}, bf16[128,192]{1,0:T(8,128)(2,1)}, u32[]{:S(2)}) copy-start(bf16[128,192]{1,0:T(8,128)(2,1)} %get-tuple-element.34) | copy-start | bytes 147460
  104.8 11.8 %copy-start.25 = (bf16[128,192]{1,0:T(8,128)(2,1)S(1)}, bf16[128,192]{1,0:T(8,128)(2,1)}, u32[]{:S(2)}) copy-start(bf16[128,192]{1,0:T(8,128)(2,1)} %get-tuple-element.37) | copy-start | bytes 147460
  112.5 7.6 %collective-permute-start.19 = (bf16[64,576]{1,0:T(8,128)(2,1)}, bf16[64,576]{1,0:T(8,128)(2,1)S(1)}, u32[]{:S(2)}, u32[]{:S(2)}) collective-permute-start(bf16[64,576]{1,0:T(8,128)(2,1)} %get-tuple-element.43), channel_id=1, source_target_pairs={{0,12},{1,13},{2,14},{3,15},{4,0},{5,1},{6,2},{7,3},{8,4},{9,5},{1... | collective-permute-start | bytes 221192 | tf_op jit(solution)/shard_map/ppermute | solution.py:25
  115.2 5.6 %collective-permute-start.21 = (bf16[64,576]{1,0:T(8,128)(2,1)}, bf16[64,576]{1,0:T(8,128)(2,1)S(1)}, u32[]{:S(2)}, u32[]{:S(2)}) collective-permute-start(bf16[64,576]{1,0:T(8,128)(2,1)} %get-tuple-element.45), channel_id=1, source_target_pairs={{0,8},{1,9},{2,10},{3,11},{4,12},{5,13},{6,14},{7,15},{8,0},{9,1},... | collective-permute-start | bytes 221192 | tf_op jit(solution)/shard_map/ppermute | solution.py:25
  115.5 4.6 %copy-start.4 = (bf16[64,576]{1,0:T(8,128)(2,1)}, bf16[64,576]{1,0:T(8,128)(2,1)S(1)}, u32[]{:S(2)}) copy-start(bf16[64,576]{1,0:T(8,128)(2,1)S(1)} %collective-permute-done.20.refs_3_) | copy-start | bytes 221188
  115.5 6.5 %collective-permute-start.23 = (bf16[64,576]{1,0:T(8,128)(2,1)}, bf16[64,576]{1,0:T(8,128)(2,1)S(1)}, u32[]{:S(2)}, u32[]{:S(2)}) collective-permute-start(bf16[64,576]{1,0:T(8,128)(2,1)} %get-tuple-element.47), channel_id=1, source_target_pairs={{0,4},{1,5},{2,6},{3,7},{4,8},{5,9},{6,10},{7,11},{8,12},{9,13},{1... | collective-permute-start | bytes 221192 | tf_op jit(solution)/shard_map/ppermute | solution.py:25
  120.1 1.9 %copy-start.5 = (bf16[64,576]{1,0:T(8,128)(2,1)}, bf16[64,576]{1,0:T(8,128)(2,1)S(1)}, u32[]{:S(2)}) copy-start(bf16[64,576]{1,0:T(8,128)(2,1)S(1)} %collective-permute-done.22.refs_5_) | copy-start | bytes 221188
  120.1 1.9 %copy-start.6 = (bf16[64,576]{1,0:T(8,128)(2,1)}, bf16[64,576]{1,0:T(8,128)(2,1)S(1)}, u32[]{:S(2)}) copy-start(bf16[64,576]{1,0:T(8,128)(2,1)S(1)} %collective-permute-done.24.refs_7_) | copy-start | bytes 221188
  120.1 1.9 %copy-start.7 = (bf16[64,576]{1,0:T(8,128)(2,1)}, bf16[64,576]{1,0:T(8,128)(2,1)S(1)}, u32[]{:S(2)}) copy-start(bf16[64,576]{1,0:T(8,128)(2,1)S(1)} %collective-permute-done.19.refs_2_) | copy-start | bytes 221188
  (6 other events, 5.5 us)
